TPU v7x, 32 devices: a whole 2x2x4 slice. The times are simulated.
32 devices in a mesh: dp: 8 (over z, x), mp: 4 (over y, core).
Axes of the slice: x: 2, y: 2, z: 4, core: 2. Of those that a mesh axis runs over, the one named last changes fastest.
Arguments:
- acts: bfloat16 [2048, 4096], P('dp'), may hold values from -6 to 6
- cotangent: bfloat16 [2048, 2048], P('dp', 'mp'), may hold values from -0.13183594 to 0.13183594
- stats: float32 [4, 8, 2, 512, 512], P('mp', 'dp'), as said below
- owner_slot: int32 [8], replicated, may hold values from 0 to 7, as said below
Outputs:
- update: bfloat16 [8, 512, 2048], P(None, 'dp', 'mp')
- new_stats: float32 [4, 8, 2, 512, 512], P('mp', 'dp')
Inputs may be any that keep to these rules, and one draw needn't show every extreme that they name: Distinct slot numbers; row block w is held by device owner_slot[w] // 1 of dp at its position owner_slot[w] % 1; some device holds 1 block. Every stats[j, s, f] is a symmetric positive definite matrix.
All inputs are finite; a program needn't handle non-finite values.
Results may differ from a plain program's by a relative error of at most 0.012.
The roundings to bfloat16 on the way count: a program that leaves them out, or rounds other values in their place, can miss the bound.
Values may be sent and summed in bfloat16 or wider, within the bound.
A program may use at most 192 MiB of HBM per device.

v0:
```python
import jax
import jax.numpy as jnp
from jax import lax
from jax.experimental import pallas as pl
from jax.experimental.pallas import tpu as pltpu
from jax.sharding import PartitionSpec as P

ITERS = 5


BETA = 0.9
DAMPING = 0.001
EPSILON = 1e-06


def batched(former, latter):
    return jnp.einsum(
        "kij,kjl->kil",
        former.astype(jnp.bfloat16),
        latter.astype(jnp.bfloat16),
        preferred_element_type=jnp.float32,
    )


def inverse_roots(stat_pair):
    identity = jnp.eye(stat_pair.shape[-1], dtype=jnp.float32)
    damped = stat_pair + DAMPING * identity
    frob_norm = jnp.sqrt(jnp.sum(damped * damped, axis=(1, 2), keepdims=True) + EPSILON)
    moment = damped / frob_norm
    result = jnp.broadcast_to(identity, stat_pair.shape)
    for iteration in range(ITERS):
        factor = (5.0 * identity - moment) * 0.25
        if iteration == 0:
            result = factor
        else:
            result = batched(result, factor)
        if iteration + 1 < ITERS:
            square = batched(factor, factor)
            moment = batched(square, batched(square, moment))
    return result * frob_norm ** (-0.25)


def precondition(grad_block, stat_pair):
    gram_left = lax.dot_general(
        grad_block, grad_block, (((1,), (1,)), ((), ())), preferred_element_type=jnp.float32
    )
    gram_right = lax.dot_general(
        grad_block, grad_block, (((0,), (0,)), ((), ())), preferred_element_type=jnp.float32
    )
    new_pair = BETA * stat_pair + (1.0 - BETA) * jnp.stack([gram_left, gram_right])
    root_pair = inverse_roots(new_pair)
    left_applied = jnp.dot(
        root_pair[0].astype(jnp.bfloat16), grad_block, preferred_element_type=jnp.float32
    )
    direction = jnp.dot(
        left_applied.astype(jnp.bfloat16),
        root_pair[1].astype(jnp.bfloat16),
        preferred_element_type=jnp.float32,
    )
    grad_wide = grad_block.astype(jnp.float32)
    graft_ratio = jnp.sqrt(
        (jnp.mean(grad_wide * grad_wide) + EPSILON) / (jnp.mean(direction * direction) + EPSILON)
    )
    return ((direction * graft_ratio).astype(jnp.bfloat16), new_pair)


def keep_slot(grad_block, stat_pair):
    return (jnp.zeros_like(grad_block), stat_pair)


def on_device(acts, cotangent, stats, owner_slot):
    dp_count = lax.axis_size("dp")
    my_index = lax.axis_index("dp")
    blk_size = cotangent.shape[1]
    blocks = acts.shape[1] // blk_size
    slot_count = stats.shape[1]
    piece_rows = blk_size // dp_count
    split_acts = acts.reshape(acts.shape[0], blocks, blk_size)
    my_slots = my_index * slot_count + jnp.arange(slot_count, dtype=jnp.int32)
    holds_block = owner_slot[None, :] == my_slots[:, None]
    filled = jnp.any(holds_block, axis=1)
    my_rows = lax.psum_scatter(
        jnp.einsum("twr,tc->rwc", split_acts, cotangent, preferred_element_type=jnp.float32),
        "dp",
        scatter_dimension=0,
        tiled=True,
    ).astype(jnp.bfloat16)
    slot_ids = jnp.arange(dp_count * slot_count, dtype=jnp.int32)
    selector = (owner_slot[None, :] == slot_ids[:, None]).astype(jnp.bfloat16)
    outgoing = jnp.einsum(
        "sw,rwc->src", selector, my_rows, preferred_element_type=jnp.float32
    ).astype(jnp.bfloat16)
    outgoing = outgoing.reshape(dp_count, slot_count, piece_rows, blk_size)
    arrived = lax.all_to_all(outgoing, "dp", split_axis=0, concat_axis=2, tiled=True)
    owned_grads = arrived.reshape(slot_count, blk_size, blk_size)
    slot_update, slot_stats = lax.cond(
        filled[0], precondition, keep_slot, owned_grads[0], stats[0, 0]
    )
    update_list = [slot_update]
    stat_list = [slot_stats]
    updates = jnp.stack(update_list)
    new_stats = jnp.stack(stat_list)[None]
    outgoing_rows = updates.reshape(slot_count, dp_count, piece_rows, blk_size)
    returned = lax.all_to_all(outgoing_rows, "dp", split_axis=1, concat_axis=1, tiled=True)
    grid_ids = (
        jnp.arange(slot_count, dtype=jnp.int32)[:, None]
        + slot_count * jnp.arange(dp_count, dtype=jnp.int32)[None, :]
    )
    picker = (owner_slot[:, None, None] == grid_ids[None]).astype(jnp.bfloat16)
    result = jnp.einsum(
        "wsn,snrc->wrc", picker, returned, preferred_element_type=jnp.float32
    ).astype(jnp.bfloat16)
    return (result, new_stats)


MESH = pl.DeviceIdType.MESH
LANES = 2
CHUNKS = 2


def gather_kernel(block_ref, acts_ref, cot_ref, grad_ref, stage, acts_all, cot_all, total,
                  a_send, a_recv, sib_send, sib_recv, y_send, y_recv, fwd_send, fwd_recv,
                  own_send, z_send, x_send, c_recv, load_sem, quarters, wholes):
    dp_count, tokens, blk = acts_all.shape
    mp_count = lax.axis_size("mp")
    part = tokens // mp_count
    chunk = tokens // CHUNKS
    depth = dp_count // LANES
    me = lax.axis_index("dp")
    mine = lax.axis_index("mp")
    z, x = me // LANES, me % LANES
    sibling = mine + 1 - 2 * (mine % 2)
    beside = (mine + 2) % mp_count
    my_rows = pl.ds(pl.multiple_of(mine * part, part), part)
    beside_rows = pl.ds(pl.multiple_of(beside * part, part), part)
    others = [(me + step) % dp_count for step in range(1, dp_count)]
    greeted = [(d, mine) for d in others] + [(me, sibling), (me, beside)]

    barrier = pltpu.get_barrier_semaphore()
    for d, m in greeted:
        pl.semaphore_signal(barrier, inc=1, device_id={"dp": d, "mp": m}, device_id_type=MESH)

    quarter_loads, whole_loads = [], []
    for w in range(dp_count):
        cols = pl.ds(w * blk, blk)
        quarter_loads.append(pltpu.make_async_copy(acts_ref.at[my_rows, cols], quarters.at[w], load_sem.at[0, w]))
        whole_loads.append(pltpu.make_async_copy(acts_ref.at[:, cols], wholes.at[w], load_sem.at[1, w]))
    for load in quarter_loads + whole_loads:
        load.start()
    for load in quarter_loads:
        load.wait()
    for d in range(dp_count):
        stage[d] = quarters[block_ref[d]]
    for load in whole_loads:
        load.wait()
    acts_all[me] = wholes[block_ref[me]]
    pl.semaphore_wait(barrier, len(greeted))

    def remote(src, dst, send, recv, d, m):
        return pltpu.make_async_remote_copy(
            src_ref=src, dst_ref=dst, send_sem=send, recv_sem=recv,
            device_id={"dp": d, "mp": m}, device_id_type=MESH)

    def acts_out(d):
        return remote(stage.at[d], acts_all.at[me, my_rows], a_send.at[d], a_recv.at[me], d, mine)

    def arrived(ref, sem):
        pltpu.make_async_copy(ref, ref, sem).wait()

    def rows_of(c):
        return pl.ds(c * chunk, chunk)

    def cot_piece(who, c):
        return cot_all.at[who, rows_of(c)]

    def own_out(way, c):
        target = (me + 1 - 2 * x, me + LANES, me - LANES)[way]
        return remote(cot_ref.at[rows_of(c)], cot_piece(me, c), own_send.at[way, c],
                      c_recv.at[me, c], target, mine)

    def z_out(zz, sign, c):
        who = zz * LANES + x
        return remote(cot_piece(who, c), cot_piece(who, c), z_send.at[zz, c], c_recv.at[who, c],
                      me + sign * LANES, mine)

    def x_out(zz, c):
        who = zz * LANES + x
        return remote(cot_piece(who, c), cot_piece(who, c), x_send.at[zz, c], c_recv.at[who, c],
                      me + 1 - 2 * x, mine)

    def side_out(s, which):
        if which == 0:
            return remote(acts_all.at[s, my_rows], acts_all.at[s, my_rows], sib_send.at[s],
                          sib_recv.at[s], me, sibling)
        if which == 1:
            return remote(acts_all.at[s, my_rows], acts_all.at[s, my_rows], y_send.at[s],
                          y_recv.at[s], me, beside)
        return remote(acts_all.at[s, beside_rows], acts_all.at[s, beside_rows], fwd_send.at[s],
                      fwd_recv.at[s], me, sibling)

    far_first = sorted(range(1, dp_count), key=lambda step: -min(step, dp_count - step))
    ordered = [(me + step) % dp_count for step in far_first]
    senders = [(me + dp_count - step) % dp_count for step in far_first]

    def own_everywhere(act):
        for c in range(CHUNKS):
            pl.when(z + 1 < depth)(lambda c=c: act(own_out(1, c)))
            pl.when(z > 0)(lambda c=c: act(own_out(2, c)))
            act(own_out(0, c))

    own_everywhere(lambda copy: copy.start())
    for d in ordered:
        acts_out(d).start()

    def relay(zz, sign, c):
        who = zz * LANES + x
        arrived(cot_piece(who, c), c_recv.at[who, c])
        nxt = z + sign
        pl.when(jnp.logical_and(nxt >= 0, nxt < depth))(lambda: z_out(zz, sign, c).start())
        x_out(zz, c).start()

    def relays(k):
        for c in range(CHUNKS):
            pl.when(z - k >= 0)(lambda c=c: relay(z - k, 1, c))
            pl.when(z + k < depth)(lambda c=c: relay(z + k, -1, c))

    def add_term(s, cot, first=False):
        term = lax.dot_general(acts_all[s], cot, (((0,), (0,)), ((), ())),
                               preferred_element_type=jnp.float32)
        total[...] = term if first else total[...] + term

    add_term(me, cot_ref[...], True)
    relays(1)
    for s in senders:
        arrived(acts_all.at[s, my_rows], a_recv.at[s])
        side_out(s, 0).start()
        side_out(s, 1).start()
    for k in range(2, depth):
        relays(k)
    for s in senders:
        arrived(acts_all.at[s, beside_rows], y_recv.at[s])
        side_out(s, 2).start()
    across = beside + 1 - 2 * (beside % 2)
    sibling_rows = pl.ds(pl.multiple_of(sibling * part, part), part)
    across_rows = pl.ds(pl.multiple_of(across * part, part), part)

    def acts_ready(s):
        arrived(acts_all.at[s, sibling_rows], sib_recv.at[s])
        arrived(acts_all.at[s, across_rows], fwd_recv.at[s])

    for k in range(1, depth):
        s = ((z + k) % depth) * LANES + x
        acts_ready(s)
        add_term(s, cot_all[s])
    for k in range(depth):
        s = ((z + k) % depth) * LANES + 1 - x
        acts_ready(s)
        for c in range(CHUNKS):
            arrived(cot_piece(s, c), c_recv.at[s, c])
        add_term(s, cot_all[s])
    grad_ref[...] = total[...].astype(grad_ref.dtype)

    own_everywhere(lambda copy: copy.wait_send())
    for d in ordered:
        acts_out(d).wait_send()
    for s in senders:
        for which in range(3):
            side_out(s, which).wait_send()

    def relay_sent(zz, sign, c):
        nxt = z + sign
        pl.when(jnp.logical_and(nxt >= 0, nxt < depth))(lambda: z_out(zz, sign, c).wait_send())
        x_out(zz, c).wait_send()

    for k in range(1, depth):
        for c in range(CHUNKS):
            pl.when(z - k >= 0)(lambda c=c, k=k: relay_sent(z - k, 1, c))
            pl.when(z + k < depth)(lambda c=c, k=k: relay_sent(z + k, -1, c))


def gather_gradient(slot_block, acts, cotangent, dp_count, mp_count):
    tokens, blk = cotangent.shape
    dma = pltpu.SemaphoreType.DMA
    depth = dp_count // LANES
    vmem = pl.BlockSpec(memory_space=pltpu.VMEM)
    return pl.pallas_call(
        gather_kernel,
        name="gather_gradient",
        out_shape=jax.ShapeDtypeStruct((blk, blk), jnp.bfloat16),
        in_specs=[pl.BlockSpec(memory_space=pltpu.SMEM), pl.BlockSpec(memory_space=pl.ANY), vmem],
        out_specs=vmem,
        scratch_shapes=[
            pltpu.VMEM((dp_count, tokens // mp_count, blk), jnp.bfloat16),
            pltpu.VMEM((dp_count, tokens, blk), jnp.bfloat16),
            pltpu.VMEM((dp_count, tokens, blk), jnp.bfloat16),
            pltpu.VMEM((blk, blk), jnp.float32),
        ] + [dma((dp_count,))] * 8 + [dma((3, CHUNKS)), dma((depth, CHUNKS)), dma((depth, CHUNKS)),
                                     dma((dp_count, CHUNKS)), dma((2, dp_count)),
                                     pltpu.VMEM((dp_count, tokens // mp_count, blk), jnp.bfloat16),
                                     pltpu.VMEM((dp_count, tokens, blk), jnp.bfloat16)],
        compiler_params=pltpu.CompilerParams(collective_id=0, has_side_effects=True),
    )(slot_block, acts, cotangent)


def mm(former, latter):
    return jnp.dot(former, latter, preferred_element_type=jnp.float32)


def root_kernel(grad_ref, stat_ref, dir_ref, new_ref):
    low = jnp.bfloat16
    blk = grad_ref.shape[0]
    grad = grad_ref[...]
    row = lax.broadcasted_iota(jnp.int32, (blk, blk), 0)
    col = lax.broadcasted_iota(jnp.int32, (blk, blk), 1)
    diagonal = row == col
    grams = [
        lax.dot_general(grad, grad, (((1,), (1,)), ((), ())), preferred_element_type=jnp.float32),
        lax.dot_general(grad, grad, (((0,), (0,)), ((), ())), preferred_element_type=jnp.float32),
    ]
    moments, results, scales = [], [None, None], []
    for side in range(2):
        fresh = BETA * stat_ref[side] + (1.0 - BETA) * grams[side]
        new_ref[side] = fresh
        damped = fresh + jnp.where(diagonal, DAMPING, 0.0)
        frob = jnp.sqrt(jnp.sum(damped * damped, axis=(0, 1), keepdims=True) + EPSILON)
        scales.append(lax.rsqrt(jnp.sqrt(frob)))
        moments.append(damped * (1.0 / frob))
    for iteration in range(ITERS):
        factors = [(jnp.where(diagonal, 5.0, 0.0) - moments[side]) * 0.25 for side in range(2)]
        lows = [factors[side].astype(low) for side in range(2)]
        if iteration + 1 < ITERS:
            squares = [mm(lows[side], lows[side]).astype(low) for side in range(2)]
            inner = [mm(squares[side], moments[side].astype(low)).astype(low) for side in range(2)]
            moments = [mm(squares[side], inner[side]) for side in range(2)]
        for side in range(2):
            results[side] = factors[side] if iteration == 0 else mm(results[side].astype(low), lows[side])
    roots = [(results[side] * scales[side]).astype(low) for side in range(2)]
    direction = mm(mm(roots[0], grad).astype(low), roots[1])
    wide = grad.astype(jnp.float32)
    count = blk * blk
    power = jnp.sum(wide * wide, axis=(0, 1), keepdims=True) / count + EPSILON
    reached = jnp.sum(direction * direction, axis=(0, 1), keepdims=True) / count + EPSILON
    dir_ref[...] = (direction * jnp.sqrt(power / reached)).astype(low)


def apply_roots(grad, stat_pair):
    vmem = pl.BlockSpec(memory_space=pltpu.VMEM)
    return pl.pallas_call(
        root_kernel,
        name="apply_roots",
        out_shape=(jax.ShapeDtypeStruct(grad.shape, jnp.bfloat16),
                   jax.ShapeDtypeStruct(stat_pair.shape, jnp.float32)),
        in_specs=[vmem, vmem],
        out_specs=(vmem, vmem),
    )(grad, stat_pair)


def return_kernel(owner_ref, dir_ref, out_ref, held, send, recv):
    dp_count, piece, blk = held.shape
    me = lax.axis_index("dp")
    others = [(me + step) % dp_count for step in range(1, dp_count)]
    barrier = pltpu.get_barrier_semaphore()
    for d in others:
        pl.semaphore_signal(barrier, inc=1, device_id={"dp": d}, device_id_type=MESH)
    pl.semaphore_wait(barrier, len(others))

    def rows_of(d):
        return pl.ds(pl.multiple_of(d * piece, piece), piece)

    far_first = sorted(range(1, dp_count), key=lambda step: -min(step, dp_count - step))
    copies = []
    for step in far_first:
        d = (me + step) % dp_count
        copy = pltpu.make_async_remote_copy(
            src_ref=dir_ref.at[rows_of(d)], dst_ref=held.at[me], send_sem=send.at[d],
            recv_sem=recv.at[me], device_id={"dp": d}, device_id_type=MESH)
        copy.start()
        copies.append(copy)
    held[me] = dir_ref[rows_of(me)]
    for d in others:
        pltpu.make_async_copy(held.at[d], held.at[d], recv.at[d]).wait()
    for w in range(dp_count):
        out_ref[w] = held[owner_ref[w]]
    for copy in copies:
        copy.wait_send()


def return_rows(owner_slot, direction, dp_count):
    blk = direction.shape[0]
    shape = (dp_count, blk // dp_count, blk)
    vmem = pl.BlockSpec(memory_space=pltpu.VMEM)
    dma = pltpu.SemaphoreType.DMA
    return pl.pallas_call(
        return_kernel,
        name="return_rows",
        out_shape=jax.ShapeDtypeStruct(shape, jnp.bfloat16),
        in_specs=[pl.BlockSpec(memory_space=pltpu.SMEM), vmem],
        out_specs=vmem,
        scratch_shapes=[pltpu.VMEM(shape, jnp.bfloat16), dma((dp_count,)), dma((dp_count,))],
        compiler_params=pltpu.CompilerParams(collective_id=1, has_side_effects=True),
    )(owner_slot, direction)


def full_house(acts, cotangent, stats, owner_slot):
    dp_count, mp_count = lax.axis_size("dp"), lax.axis_size("mp")
    ids = jnp.arange(dp_count, dtype=jnp.int32)
    slot_block = jnp.sum(jnp.where(owner_slot[None, :] == ids[:, None], ids[None, :], 0), axis=1)
    grad = gather_gradient(slot_block, acts, cotangent, dp_count, mp_count)
    direction, new_pair = apply_roots(grad, stats[0, 0])
    return return_rows(owner_slot, direction, dp_count), new_pair[None, None]


def device_body(acts, cotangent, stats, owner_slot):
    dp_count, mp_count = lax.axis_size("dp"), lax.axis_size("mp")
    blk = cotangent.shape[1]
    every_slot_filled = stats.shape[1] == 1 and acts.shape[1] == dp_count * blk
    if every_slot_filled and mp_count == 4 and dp_count % LANES == 0 and dp_count <= 8:
        return full_house(acts, cotangent, stats, owner_slot)
    return on_device(acts, cotangent, stats, owner_slot)


def solution(mesh):
    return jax.shard_map(
        device_body,
        mesh=mesh,
        in_specs=(P("dp", None), P("dp", "mp"), P("mp", "dp", None, None, None), P()),
        out_specs=(P(None, "dp", "mp"), P("mp", "dp", None, None, None)),
        check_vma=False,
    )
```

profile of v0, /device:TPU:0, one launch (start us, length us, event | category | flops | bytes accessed | tf_op | source)
XLA Modules:
  0.0 74.6 jit_solution(170046323263222442)
XLA Ops:
  0.6 1.3 %select_reduce_fusion.block_ref = s32[8]{0:T(128)} fusion(s32[8]{0:T(128)} %owner_ref.1), kind=kLoop, calls=%fused_computation | loop fusion | flops 184 | bytes 64 | tf_op jit(solution)/shard_map/reduce_sum | solution.py:407
  1.9 42.0 %gather_gradient.1.grad_ref = bf16[512,512]{1,0:T(8,128)(2,1)} custom-call(s32[8]{0:T(128)} %select_reduce_fusion.block_ref, bf16[256,4096]{1,0:T(8,128)(2,1)} %acts_ref.1, bf16[256,512]{1,0:T(8,128)(2,1)} %cot_ref.1), custom_call_target="tpu_custom_call" | custom-call | tf_op jit(solution)/shard_map/gather_gradient/pallas_call | solution.py:286
  43.9 13.6 %apply_roots.1 = (bf16[512,512]{1,0:T(8,128)(2,1)}, f32[2,512,512]{2,1,0:T(8,128)}) custom-call(bf16[512,512]{1,0:T(8,128)(2,1)} %gather_gradient.1.grad_ref, f32[2,512,512]{2,1,0:T(8,128)} %bitcast.2), custom_call_target="tpu_custom_call" | custom-call | tf_op jit(solution)/shard_map/apply_roots/pallas_call | solution.py:348
  57.5 15.2 %return_rows.1 = bf16[8,64,512]{2,1,0:T(8,128)(2,1)} custom-call(s32[8]{0:T(128)} %owner_ref.1, bf16[512,512]{1,0:T(8,128)(2,1)} %get-tuple-element.4.dir_ref), custom_call_target="tpu_custom_call" | custom-call | tf_op jit(solution)/shard_map/return_rows/pallas_call | solution.py:393
  72.7 1.9 %copy.7 = bf16[8,64,512]{2,1,0:T(8,128)(2,1)} copy(bf16[8,64,512]{2,1,0:T(8,128)(2,1)} %return_rows.1) | data formatting | bytes 1048576
where the time goes:
time: 74.8 us; the launch traced here: 74.6 us
  Pallas kernels  70.8 us (95%)
  local copies, waits for them, and re-layouts  1.87 us (2%)
  other arithmetic  1.28 us (2%)
    pallas_call x1, Pallas kernels, gather_gradient(): pl.pallas_call(gather_kernel, name='gather_gradient', out_shape=jax.Shape...  42 us
    pallas_call x1, Pallas kernels, return_rows(): pl.pallas_call(return_kernel, name='return_rows', out_shape=jax.ShapeDtyp...  15.2 us
    pallas_call x1, Pallas kernels, apply_roots(): pl.pallas_call(root_kernel, name='apply_roots', out_shape=(jax.ShapeDtype...  13.6 us
    unnamed x1, local copies, waits for them, and re-layouts  1.87 us

commit v1 on v0

v1 whole, which is shorter than its diff:
```python
import jax
import jax.numpy as jnp
from jax import lax
from jax.experimental import pallas as pl
from jax.experimental.pallas import tpu as pltpu
from jax.sharding import PartitionSpec as P

ITERS = 5


BETA = 0.9
DAMPING = 0.001
EPSILON = 1e-06


def batched(former, latter):
    return jnp.einsum(
        "kij,kjl->kil",
        former.astype(jnp.bfloat16),
        latter.astype(jnp.bfloat16),
        preferred_element_type=jnp.float32,
    )


def inverse_roots(stat_pair):
    identity = jnp.eye(stat_pair.shape[-1], dtype=jnp.float32)
    damped = stat_pair + DAMPING * identity
    frob_norm = jnp.sqrt(jnp.sum(damped * damped, axis=(1, 2), keepdims=True) + EPSILON)
    moment = damped / frob_norm
    result = jnp.broadcast_to(identity, stat_pair.shape)
    for iteration in range(ITERS):
        factor = (5.0 * identity - moment) * 0.25
        if iteration == 0:
            result = factor
        else:
            result = batched(result, factor)
        if iteration + 1 < ITERS:
            square = batched(factor, factor)
            moment = batched(square, batched(square, moment))
    return result * frob_norm ** (-0.25)


def precondition(grad_block, stat_pair):
    gram_left = lax.dot_general(
        grad_block, grad_block, (((1,), (1,)), ((), ())), preferred_element_type=jnp.float32
    )
    gram_right = lax.dot_general(
        grad_block, grad_block, (((0,), (0,)), ((), ())), preferred_element_type=jnp.float32
    )
    new_pair = BETA * stat_pair + (1.0 - BETA) * jnp.stack([gram_left, gram_right])
    root_pair = inverse_roots(new_pair)
    left_applied = jnp.dot(
        root_pair[0].astype(jnp.bfloat16), grad_block, preferred_element_type=jnp.float32
    )
    direction = jnp.dot(
        left_applied.astype(jnp.bfloat16),
        root_pair[1].astype(jnp.bfloat16),
        preferred_element_type=jnp.float32,
    )
    grad_wide = grad_block.astype(jnp.float32)
    graft_ratio = jnp.sqrt(
        (jnp.mean(grad_wide * grad_wide) + EPSILON) / (jnp.mean(direction * direction) + EPSILON)
    )
    return ((direction * graft_ratio).astype(jnp.bfloat16), new_pair)


def keep_slot(grad_block, stat_pair):
    return (jnp.zeros_like(grad_block), stat_pair)


def on_device(acts, cotangent, stats, owner_slot):
    dp_count = lax.axis_size("dp")
    my_index = lax.axis_index("dp")
    blk_size = cotangent.shape[1]
    blocks = acts.shape[1] // blk_size
    slot_count = stats.shape[1]
    piece_rows = blk_size // dp_count
    split_acts = acts.reshape(acts.shape[0], blocks, blk_size)
    my_slots = my_index * slot_count + jnp.arange(slot_count, dtype=jnp.int32)
    holds_block = owner_slot[None, :] == my_slots[:, None]
    filled = jnp.any(holds_block, axis=1)
    my_rows = lax.psum_scatter(
        jnp.einsum("twr,tc->rwc", split_acts, cotangent, preferred_element_type=jnp.float32),
        "dp",
        scatter_dimension=0,
        tiled=True,
    ).astype(jnp.bfloat16)
    slot_ids = jnp.arange(dp_count * slot_count, dtype=jnp.int32)
    selector = (owner_slot[None, :] == slot_ids[:, None]).astype(jnp.bfloat16)
    outgoing = jnp.einsum(
        "sw,rwc->src", selector, my_rows, preferred_element_type=jnp.float32
    ).astype(jnp.bfloat16)
    outgoing = outgoing.reshape(dp_count, slot_count, piece_rows, blk_size)
    arrived = lax.all_to_all(outgoing, "dp", split_axis=0, concat_axis=2, tiled=True)
    owned_grads = arrived.reshape(slot_count, blk_size, blk_size)
    slot_update, slot_stats = lax.cond(
        filled[0], precondition, keep_slot, owned_grads[0], stats[0, 0]
    )
    update_list = [slot_update]
    stat_list = [slot_stats]
    updates = jnp.stack(update_list)
    new_stats = jnp.stack(stat_list)[None]
    outgoing_rows = updates.reshape(slot_count, dp_count, piece_rows, blk_size)
    returned = lax.all_to_all(outgoing_rows, "dp", split_axis=1, concat_axis=1, tiled=True)
    grid_ids = (
        jnp.arange(slot_count, dtype=jnp.int32)[:, None]
        + slot_count * jnp.arange(dp_count, dtype=jnp.int32)[None, :]
    )
    picker = (owner_slot[:, None, None] == grid_ids[None]).astype(jnp.bfloat16)
    result = jnp.einsum(
        "wsn,snrc->wrc", picker, returned, preferred_element_type=jnp.float32
    ).astype(jnp.bfloat16)
    return (result, new_stats)


MESH = pl.DeviceIdType.MESH
LANES = 2
DEPTH = 4
CHUNKS = 4
END_ORDER = (
    "O2", "a0x", "a1=", "O1", "a2x", "O0", "O3", "A1=", "A0x", "A2x", "R10", "R11",
    "a1x", "R12", "R21", "M0x", "a3x", "A1x", "a2=", "R31", "A2=", "R20", "R13", "a3=",
    "R22", "A3x", "M1=", "R23", "R30", "A3=", "R33", "M2x", "M1x", "M2=", "R32", "M3=",
    "M3x",
)
INNER_ORDER = (
    "O3", "a0=", "a2=", "O1", "a1x", "a3x", "O2", "O0", "R01", "a0x", "a3=", "A1x",
    "R21", "A2=", "R00", "A3x", "a2x", "R03", "R31", "R20", "A0x", "R22", "R23", "R02",
    "A0=", "M2=", "M1x", "R30", "A2x", "R33", "A3=", "R32", "M0x", "M3=", "M0=", "M2x",
    "M3x",
)


def mm(former, latter):
    return jnp.dot(former, latter, preferred_element_type=jnp.float32)


def step_kernel(slot_ref, acts_ref, cot_ref, stat_ref, held_ref, new_ref,
                stage, quarters, wholes, acts_all, cot_all, total, stats, direction,
                a_send, a_recv, sib_send, sib_recv, y_send, y_recv, fwd_send, fwd_recv,
                own_send, z_send, x_send, c_recv, quarter_sem, whole_sem, cot_sem, stat_sem,
                back_send, back_recv, owner_ref, owner_sem):
    dp_count, tokens, blk = acts_all.shape
    mp_count = lax.axis_size("mp")
    part = tokens // mp_count
    chunk = tokens // CHUNKS
    me = lax.axis_index("dp")
    mine = lax.axis_index("mp")
    z, x = me // LANES, me % LANES
    half = z // (DEPTH // 2)
    sign = 1 - 2 * half
    level = half * (DEPTH - 1) + sign * z
    sibling = mine + 1 - 2 * (mine % 2)
    beside = (mine + 2) % mp_count
    across = beside + 1 - 2 * (beside % 2)

    def part_rows(m):
        return pl.ds(pl.multiple_of(m * part, part), part)

    my_rows, beside_rows = part_rows(mine), part_rows(beside)
    sibling_rows, across_rows = part_rows(sibling), part_rows(across)

    def line(i):
        return half * (DEPTH - 1) + sign * i

    def at(i, other):
        return line(i) * LANES + (1 - x if other else x)

    others = [(me + step) % dp_count for step in range(1, dp_count)]
    greeted = [(d, mine) for d in others] + [(me, m) for m in (sibling, beside, across)]
    barrier = pltpu.get_barrier_semaphore()
    for d, m in greeted:
        pl.semaphore_signal(barrier, inc=1, device_id={"dp": d, "mp": m}, device_id_type=MESH)

    cot_load = pltpu.make_async_copy(cot_ref, cot_all.at[me], cot_sem)
    cot_load.start()
    owner_load = pltpu.make_async_copy(slot_ref, owner_ref, owner_sem)
    owner_load.start()
    quarter_loads, whole_loads = [], []
    for w in range(dp_count):
        cols = pl.ds(w * blk, blk)
        quarter_loads.append(pltpu.make_async_copy(acts_ref.at[my_rows, cols], quarters.at[w], quarter_sem.at[w]))
        whole_loads.append(pltpu.make_async_copy(acts_ref.at[:, cols], wholes.at[w], whole_sem.at[w]))
    stat_load = pltpu.make_async_copy(stat_ref, stats, stat_sem)
    for load in quarter_loads + whole_loads + [stat_load]:
        load.start()

    def block_of(d):
        found = 0
        for w in range(dp_count):
            found = jnp.where(owner_ref[w] == d, w, found)
        return found

    def remote(src, dst, send, recv, d, m):
        return pltpu.make_async_remote_copy(
            src_ref=src, dst_ref=dst, send_sem=send, recv_sem=recv,
            device_id={"dp": d, "mp": m}, device_id_type=MESH)

    def arrived(ref, sem):
        pltpu.make_async_copy(ref, ref, sem).wait()

    def cot_piece(who, c):
        return cot_all.at[who, pl.ds(c * chunk, chunk)]

    def own_out(way, c, target):
        return remote(cot_piece(me, c), cot_piece(me, c), own_send.at[way, c], c_recv.at[me, c], target, mine)

    def z_out(i, to, c):
        who = at(i, False)
        return remote(cot_piece(who, c), cot_piece(who, c), z_send.at[i, c], c_recv.at[who, c], at(to, False), mine)

    def x_out(i, c):
        who = at(i, False)
        return remote(cot_piece(who, c), cot_piece(who, c), x_send.at[i, c], c_recv.at[who, c], me + 1 - 2 * x, mine)

    def acts_out(d):
        return remote(stage.at[d], acts_all.at[me, my_rows], a_send.at[d], a_recv.at[me], d, mine)

    def side_out(s, side):
        piece = acts_all.at[s, my_rows]
        return remote(piece, piece, (sib_send, y_send, fwd_send)[side].at[s], (sib_recv, y_recv, fwd_recv)[side].at[s],
                      me, (sibling, beside, across)[side])

    def own_outs(lev, c):
        copies = [own_out(0, c, at(lev + 1, False))]
        if lev > 0:
            copies.append(own_out(1, c, at(lev - 1, False)))
        return copies + [own_out(2, c, me + 1 - 2 * x)]

    def relays(lev, i, c):
        copies = [x_out(i, c)]
        if lev > 0:
            copies.append(z_out(i, lev + 1 if i < lev else lev - 1, c))
        return copies

    def by_level(act):
        for lev in range(DEPTH // 2):
            @pl.when(level == lev)
            def _(lev=lev):
                act(lev)

    def start(copies):
        for copy in copies:
            copy.start()

    def handle(word, lev):
        kind, i, which = word[0], int(word[1]), word[2:]
        if kind == "O":
            start(own_outs(lev, i))
        elif kind == "R":
            who = at(i, False)
            arrived(cot_piece(who, int(which)), c_recv.at[who, int(which)])
            start(relays(lev, i, int(which)))
        else:
            s = at(i, which == "x")
            if kind == "a":
                start([acts_out(s)])
            elif kind == "A":
                arrived(acts_all.at[s, my_rows], a_recv.at[s])
                start([side_out(s, side) for side in (1, 2, 0)])
            else:
                arrived(acts_all.at[s, sibling_rows], sib_recv.at[s])
                arrived(acts_all.at[s, beside_rows], y_recv.at[s])
                arrived(acts_all.at[s, across_rows], fwd_recv.at[s])
                if which == "x":
                    for c in range(CHUNKS):
                        arrived(cot_piece(s, c), c_recv.at[s, c])

    def parts_of(order):
        head = next(n for n, word in enumerate(order) if word[0] != "O")
        wait = next(n for n, word in enumerate(order) if word[0] in "RAM")
        found, now = [order[:head], order[head:wait]], []
        for word in order[wait:]:
            now.append(word)
            if word[0] == "M":
                found.append(now)
                now = []
        return found

    plans = [parts_of(END_ORDER), parts_of(INNER_ORDER)]

    def run_part(n):
        by_level(lambda lev: [handle(word, lev) for word in plans[lev][n]])

    def blend(end, inner):
        return end + (inner - end) * level

    def term_of(n):
        words = [plan[n][-1] for plan in plans]
        place = blend(*[int(word[1]) for word in words])
        other = blend(*[int(word[2] == "x") for word in words])
        return line(place) * LANES + x + (1 - 2 * x) * other

    def product(s):
        return lax.dot_general(acts_all[s], cot_all[s], (((0,), (0,)), ((), ())),
                               preferred_element_type=jnp.float32)

    cot_load.wait()
    pl.semaphore_wait(barrier, len(greeted))
    run_part(0)
    for load in quarter_loads + [owner_load]:
        load.wait()
    for d in range(dp_count):
        stage[d] = quarters[block_of(d)]
    run_part(1)
    for load in whole_loads:
        load.wait()
    acts_all[me] = wholes[block_of(me)]
    total[...] = product(me)
    for n in range(2, dp_count + 1):
        run_part(n)
        total[...] = total[...] + product(term_of(n))

    grad = total[...].astype(jnp.bfloat16)
    stat_load.wait()
    direction[...] = precondition_block(grad, stats, new_ref)

    def rows_of(d):
        return pl.ds(pl.multiple_of(d * held_ref.shape[1], held_ref.shape[1]), held_ref.shape[1])

    copies = []
    for step in sorted(range(1, dp_count), key=lambda step: -min(step, dp_count - step)):
        d = (me + step) % dp_count
        copies.append(remote(direction.at[rows_of(d)], held_ref.at[me], back_send.at[d], back_recv.at[me], d, mine))
        copies[-1].start()
    held_ref[me] = direction[rows_of(me)]

    def sent(lev):
        for c in range(CHUNKS):
            for copy in own_outs(lev, c) + [copy for i in range(DEPTH) if i != lev for copy in relays(lev, i, c)]:
                copy.wait_send()

    by_level(sent)
    for s in others:
        acts_out(s).wait_send()
        for side in range(3):
            side_out(s, side).wait_send()
    for d in others:
        arrived(held_ref.at[d], back_recv.at[d])
    for copy in copies:
        copy.wait_send()


def precondition_block(grad, stat_ref, new_ref):
    low = jnp.bfloat16
    blk = grad.shape[0]
    row = lax.broadcasted_iota(jnp.int32, (blk, blk), 0)
    col = lax.broadcasted_iota(jnp.int32, (blk, blk), 1)
    diagonal = row == col
    grams = [
        lax.dot_general(grad, grad, (((1,), (1,)), ((), ())), preferred_element_type=jnp.float32),
        lax.dot_general(grad, grad, (((0,), (0,)), ((), ())), preferred_element_type=jnp.float32),
    ]
    moments, results, scales = [], [None, None], []
    for side in range(2):
        fresh = BETA * stat_ref[side] + (1.0 - BETA) * grams[side]
        new_ref[side] = fresh
        damped = fresh + jnp.where(diagonal, DAMPING, 0.0)
        frob = jnp.sqrt(jnp.sum(damped * damped, axis=(0, 1), keepdims=True) + EPSILON)
        scales.append(lax.rsqrt(jnp.sqrt(frob)))
        moments.append(damped * (1.0 / frob))
    for iteration in range(ITERS):
        factors = [(jnp.where(diagonal, 5.0, 0.0) - moments[side]) * 0.25 for side in range(2)]
        lows = [factors[side].astype(low) for side in range(2)]
        if iteration + 1 < ITERS:
            squares = [mm(lows[side], lows[side]).astype(low) for side in range(2)]
            inner = [mm(squares[side], moments[side].astype(low)).astype(low) for side in range(2)]
            moments = [mm(squares[side], inner[side]) for side in range(2)]
        for side in range(2):
            results[side] = factors[side] if iteration == 0 else mm(results[side].astype(low), lows[side])
    roots = [(results[side] * scales[side]).astype(low) for side in range(2)]
    aimed = mm(mm(roots[0], grad).astype(low), roots[1])
    wide = grad.astype(jnp.float32)
    count = blk * blk
    power = jnp.sum(wide * wide, axis=(0, 1), keepdims=True) / count + EPSILON
    reached = jnp.sum(aimed * aimed, axis=(0, 1), keepdims=True) / count + EPSILON
    return (aimed * jnp.sqrt(power / reached)).astype(low)


def owned_step(owner_slot, acts, cotangent, stat_pair, dp_count, mp_count):
    tokens, blk = cotangent.shape
    low, dma = jnp.bfloat16, pltpu.SemaphoreType.DMA
    vmem, hbm = pl.BlockSpec(memory_space=pltpu.VMEM), pl.BlockSpec(memory_space=pltpu.HBM)
    return pl.pallas_call(
        step_kernel,
        name="owned_step",
        out_shape=(jax.ShapeDtypeStruct((dp_count, blk // dp_count, blk), low),
                   jax.ShapeDtypeStruct(stat_pair.shape, jnp.float32)),
        in_specs=[hbm, hbm, hbm, hbm],
        out_specs=(vmem, vmem),
        scratch_shapes=[
            pltpu.VMEM((dp_count, tokens // mp_count, blk), low),
            pltpu.VMEM((dp_count, tokens // mp_count, blk), low),
            pltpu.VMEM((dp_count, tokens, blk), low),
            pltpu.VMEM((dp_count, tokens, blk), low),
            pltpu.VMEM((dp_count, tokens, blk), low),
            pltpu.VMEM((blk, blk), jnp.float32),
            pltpu.VMEM(stat_pair.shape, jnp.float32),
            pltpu.VMEM((blk, blk), low),
        ] + [dma((dp_count,))] * 8 + [dma((3, CHUNKS)), dma((DEPTH, CHUNKS)), dma((DEPTH, CHUNKS)),
                                     dma((dp_count, CHUNKS)), dma((dp_count,)), dma((dp_count,)), dma, dma,
                                     dma((dp_count,)), dma((dp_count,)),
                                     pltpu.SMEM(owner_slot.shape, jnp.int32), dma],
        compiler_params=pltpu.CompilerParams(collective_id=0, has_side_effects=True,
                                             vmem_limit_bytes=48 * 1024 * 1024),
    )(*[pltpu.with_memory_space_constraint(a, pltpu.HBM) for a in (owner_slot, acts, cotangent, stat_pair)])


def place_kernel(owner_ref, held_ref, pair_ref, out_ref, new_ref, sems, pair_sem):
    stats_out = pltpu.make_async_copy(pair_ref, new_ref, pair_sem)
    stats_out.start()
    copies = [pltpu.make_async_copy(held_ref.at[owner_ref[w]], out_ref.at[w], sems.at[w])
              for w in range(held_ref.shape[0])]
    for copy in copies:
        copy.start()
    for copy in copies + [stats_out]:
        copy.wait()


def place_rows(owner_slot, held, new_pair):
    vmem, hbm = pl.BlockSpec(memory_space=pltpu.VMEM), pl.BlockSpec(memory_space=pltpu.HBM)
    return pl.pallas_call(
        place_kernel,
        name="place_rows",
        out_shape=(jax.ShapeDtypeStruct(held.shape, held.dtype),
                   jax.ShapeDtypeStruct(new_pair.shape, new_pair.dtype)),
        in_specs=[pl.BlockSpec(memory_space=pltpu.SMEM), vmem, vmem],
        out_specs=(hbm, hbm),
        scratch_shapes=[pltpu.SemaphoreType.DMA((held.shape[0],)), pltpu.SemaphoreType.DMA],
        compiler_params=pltpu.CompilerParams(vmem_limit_bytes=4 * 1024 * 1024),
    )(owner_slot, held, new_pair)


def full_house(acts, cotangent, stats, owner_slot):
    dp_count, mp_count = lax.axis_size("dp"), lax.axis_size("mp")
    held, new_pair = owned_step(owner_slot, acts, cotangent, stats[0, 0], dp_count, mp_count)
    update, new_pair = place_rows(owner_slot, held, new_pair)
    return update, new_pair[None, None]


def device_body(acts, cotangent, stats, owner_slot):
    dp_count, mp_count = lax.axis_size("dp"), lax.axis_size("mp")
    blk = cotangent.shape[1]
    every_slot_filled = stats.shape[1] == 1 and acts.shape[1] == dp_count * blk
    if every_slot_filled and mp_count == 4 and dp_count == LANES * DEPTH:
        return full_house(acts, cotangent, stats, owner_slot)
    return on_device(acts, cotangent, stats, owner_slot)


def solution(mesh):
    return jax.shard_map(
        device_body,
        mesh=mesh,
        in_specs=(P("dp", None), P("dp", "mp"), P("mp", "dp", None, None, None), P()),
        out_specs=(P(None, "dp", "mp"), P("mp", "dp", None, None, None)),
        check_vma=False,
    )
```

time: 74.8 us -> 62.3 us (0.83)
  Pallas kernels: 70.8 us -> 61.5 us
  local copies, waits for them, and re-layouts: 1.87 us -> 0.01 us
  other arithmetic: 1.28 us -> 0 us
    pallas_call x3 -> x2, Pallas kernels: 70.8 us -> 61.5 us  [the longest x1 59.4 us: owned_step(): pl.pallas_call(step_kernel, name='owned_step', out_shape=(jax.ShapeDtypeS...]
    unnamed x1 -> x2, local copies, waits for them, and re-layouts: 1.87 us -> 0.01 us
    reduce_sum x1 -> x0, other arithmetic: 1.28 us -> none  [full_house(): jnp.sum(jnp.where(owner_slot[None, :] == ids[:, None], ids[None, :], 0),...]
where the time goes in v1:
time: 62.3 us; the launch traced here: 62.1 us
  Pallas kernels  61.5 us (99%)
  between operations  0.65 us (1%)
    pallas_call x1, Pallas kernels, owned_step(): pl.pallas_call(step_kernel, name='owned_step', out_shape=(jax.ShapeDtypeS...  59.4 us
    pallas_call x1, Pallas kernels, place_rows(): pl.pallas_call(place_kernel, name='place_rows', out_shape=(jax.ShapeDtype...  2.09 us

profile of v1, /device:TPU:0, one launch (start us, length us, event | category | flops | bytes accessed | tf_op | source)
XLA Modules:
  0.0 62.1 jit_solution(366070939614089132)
XLA Ops:
  0.6 0.0 copy-start
  0.6 59.4 %owned_step.1 = (bf16[8,64,512]{2,1,0:T(8,128)(2,1)S(1)}, f32[2,512,512]{2,1,0:T(8,128)S(1)}) custom-call(s32[8]{0:T(128)} %owner_ref.1, bf16[256,4096]{1,0:T(8,128)(2,1)} %acts_ref.1, bf16[256,512]{1,0:T(8,128)(2,1)} %cot_ref.1, f32[2,512,512]{2,1,0:T(8,128)} %bitcast.2), custom_call_target="tpu_custom_call" | custom-call | tf_op jit(solution)/shard_map/owned_step/pallas_call | solution.py:384
  60.0 0.0 copy-done
  60.0 2.1 %place_rows.1 = (bf16[8,64,512]{2,1,0:T(8,128)(2,1)}, f32[2,512,512]{2,1,0:T(8,128)}) custom-call(s32[8]{0:T(128)S(1)} %copy-done, bf16[8,64,512]{2,1,0:T(8,128)(2,1)S(1)} %get-tuple-element.6.held_ref, f32[2,512,512]{2,1,0:T(8,128)S(1)} %get-tuple-element.7.pair_ref), custom_call_target="tpu_custom_call" | custom-call | tf_op jit(solution)/shard_map/place_rows/pallas_call | solution.py:422
Async XLA Ops:
  0.6 59.4 %copy-start = (s32[8]{0:T(128)S(1)}, s32[8]{0:T(128)}, u32[]{:S(2)}) copy-start(s32[8]{0:T(128)} %owner_ref.1) | copy-start | bytes 100

commit v2 on v1

--- a/solution.py
+++ b/solution.py
@@ -131,12 +131,15 @@
 )
 
 
+BACK_ORDER = ((3, 3), (2, 0), (1, 2), (0, 1))
+
+
 def mm(former, latter):
     return jnp.dot(former, latter, preferred_element_type=jnp.float32)
 
 
 def step_kernel(slot_ref, acts_ref, cot_ref, stat_ref, held_ref, new_ref,
-                stage, quarters, wholes, acts_all, cot_all, total, stats, direction,
+                stage, quarters, wholes, acts_all, cot_all, total, stats, direction, left_root,
                 a_send, a_recv, sib_send, sib_recv, y_send, y_recv, fwd_send, fwd_recv,
                 own_send, z_send, x_send, c_recv, quarter_sem, whole_sem, cot_sem, stat_sem,
                 back_send, back_recv, owner_ref, owner_sem):
@@ -313,16 +316,26 @@
 
     grad = total[...].astype(jnp.bfloat16)
     stat_load.wait()
-    direction[...] = precondition_block(grad, stats, new_ref)
-
-    def rows_of(d):
-        return pl.ds(pl.multiple_of(d * held_ref.shape[1], held_ref.shape[1]), held_ref.shape[1])
-
+    left_root[...], right_root = roots_of(grad, stats, new_ref)
+    piece = held_ref.shape[1]
+    wide = grad.astype(jnp.float32)
+    power, reached = jnp.sum(wide * wide, axis=(0, 1), keepdims=True), 0.0
+
+    def rows_of(d, count=1):
+        return pl.ds(pl.multiple_of(d * piece, piece), count * piece)
+
+    planes = [line(blend(*pair)) for pair in BACK_ORDER]
+    aims = []
+    for plane in planes:
+        aims.append(mm(mm(left_root[rows_of(plane * LANES, LANES)], grad).astype(jnp.bfloat16), right_root))
+        reached = reached + jnp.sum(aims[-1] * aims[-1], axis=(0, 1), keepdims=True)
+    gain = jnp.sqrt((power / wide.size + EPSILON) / (reached / wide.size + EPSILON))
     copies = []
-    for step in sorted(range(1, dp_count), key=lambda step: -min(step, dp_count - step)):
-        d = (me + step) % dp_count
-        copies.append(remote(direction.at[rows_of(d)], held_ref.at[me], back_send.at[d], back_recv.at[me], d, mine))
-        copies[-1].start()
+    for n, plane in enumerate(planes):
+        direction[rows_of(plane * LANES, LANES)] = (aims[n] * gain).astype(jnp.bfloat16)
+        for d in ([plane * LANES + lane for lane in range(LANES)] if n + 1 < DEPTH else [me + 1 - 2 * x]):
+            copies.append(remote(direction.at[rows_of(d)], held_ref.at[me], back_send.at[d], back_recv.at[me], d, mine))
+            copies[-1].start()
     held_ref[me] = direction[rows_of(me)]
 
     def sent(lev):
@@ -341,40 +354,63 @@
         copy.wait_send()
 
 
-def precondition_block(grad, stat_ref, new_ref):
+def roots_of(grad, stat_ref, new_ref):
     low = jnp.bfloat16
     blk = grad.shape[0]
-    row = lax.broadcasted_iota(jnp.int32, (blk, blk), 0)
-    col = lax.broadcasted_iota(jnp.int32, (blk, blk), 1)
+    half = blk // 2
+    row = lax.broadcasted_iota(jnp.int32, (half, half), 0)
+    col = lax.broadcasted_iota(jnp.int32, (half, half), 1)
     diagonal = row == col
-    grams = [
-        lax.dot_general(grad, grad, (((1,), (1,)), ((), ())), preferred_element_type=jnp.float32),
-        lax.dot_general(grad, grad, (((0,), (0,)), ((), ())), preferred_element_type=jnp.float32),
-    ]
+
+    def whole(parts):
+        near, cross, far = [part.astype(low) for part in parts]
+        return jnp.concatenate([jnp.concatenate([near, cross], 1), jnp.concatenate([cross.T, far], 1)], 0)
+
+    def product(former, latter):
+        top = mm(former[:half], latter)
+        return top[:, :half], top[:, half:], mm(former[half:], latter[:, half:])
+
+    def gram(rows):
+        def part(a, b):
+            return lax.dot_general(a, b, (((1,), (1,)), ((), ())), preferred_element_type=jnp.float32)
+
+        top = part(rows[:half], rows)
+        return top[:, :half], top[:, half:], part(rows[half:], rows[half:])
+
+    def gram_t(cols):
+        def part(a, b):
+            return lax.dot_general(a, b, (((0,), (0,)), ((), ())), preferred_element_type=jnp.float32)
+
+        top = part(cols[:, :half], cols)
+        return top[:, :half], top[:, half:], part(cols[:, half:], cols[:, half:])
+
+    def total_of(parts):
+        near, cross, far = [jnp.sum(part * part, axis=(0, 1), keepdims=True) for part in parts]
+        return near + 2.0 * cross + far
+
+    spots = [(slice(0, half), slice(0, half)), (slice(0, half), slice(half, blk)), (slice(half, blk), slice(half, blk))]
     moments, results, scales = [], [None, None], []
-    for side in range(2):
-        fresh = BETA * stat_ref[side] + (1.0 - BETA) * grams[side]
-        new_ref[side] = fresh
-        damped = fresh + jnp.where(diagonal, DAMPING, 0.0)
-        frob = jnp.sqrt(jnp.sum(damped * damped, axis=(0, 1), keepdims=True) + EPSILON)
+    for side, grams in enumerate((gram(grad), gram_t(grad))):
+        fresh = [BETA * stat_ref[side, r, c] + (1.0 - BETA) * part for (r, c), part in zip(spots, grams)]
+        for (r, c), part in zip(spots, fresh):
+            new_ref[side, r, c] = part
+        new_ref[side, half:, :half] = fresh[1].T
+        shift = jnp.where(diagonal, DAMPING, 0.0)
+        damped = [fresh[0] + shift, fresh[1], fresh[2] + shift]
+        frob = jnp.sqrt(total_of(damped) + EPSILON)
         scales.append(lax.rsqrt(jnp.sqrt(frob)))
-        moments.append(damped * (1.0 / frob))
+        moments.append([part * (1.0 / frob) for part in damped])
     for iteration in range(ITERS):
-        factors = [(jnp.where(diagonal, 5.0, 0.0) - moments[side]) * 0.25 for side in range(2)]
-        lows = [factors[side].astype(low) for side in range(2)]
+        five = jnp.where(diagonal, 5.0, 0.0)
+        factors = [[(five - m[0]) * 0.25, m[1] * -0.25, (five - m[2]) * 0.25] for m in moments]
+        lows = [whole(factor) for factor in factors]
         if iteration + 1 < ITERS:
-            squares = [mm(lows[side], lows[side]).astype(low) for side in range(2)]
-            inner = [mm(squares[side], moments[side].astype(low)).astype(low) for side in range(2)]
-            moments = [mm(squares[side], inner[side]) for side in range(2)]
+            squares = [whole(product(lows[side], lows[side])) for side in range(2)]
+            inner = [whole(product(squares[side], whole(moments[side]))) for side in range(2)]
+            moments = [product(squares[side], inner[side]) for side in range(2)]
         for side in range(2):
-            results[side] = factors[side] if iteration == 0 else mm(results[side].astype(low), lows[side])
-    roots = [(results[side] * scales[side]).astype(low) for side in range(2)]
-    aimed = mm(mm(roots[0], grad).astype(low), roots[1])
-    wide = grad.astype(jnp.float32)
-    count = blk * blk
-    power = jnp.sum(wide * wide, axis=(0, 1), keepdims=True) / count + EPSILON
-    reached = jnp.sum(aimed * aimed, axis=(0, 1), keepdims=True) / count + EPSILON
-    return (aimed * jnp.sqrt(power / reached)).astype(low)
+            results[side] = factors[side] if iteration == 0 else product(whole(results[side]), lows[side])
+    return [whole([part * scales[side] for part in results[side]]) for side in range(2)]
 
 
 def owned_step(owner_slot, acts, cotangent, stat_pair, dp_count, mp_count):
@@ -397,6 +433,7 @@
             pltpu.VMEM((blk, blk), jnp.float32),
             pltpu.VMEM(stat_pair.shape, jnp.float32),
             pltpu.VMEM((blk, blk), low),
+            pltpu.VMEM((blk, blk), low),
         ] + [dma((dp_count,))] * 8 + [dma((3, CHUNKS)), dma((DEPTH, CHUNKS)), dma((DEPTH, CHUNKS)),
                                      dma((dp_count, CHUNKS)), dma((dp_count,)), dma((dp_count,)), dma, dma,
                                      dma((dp_count,)), dma((dp_count,)),

time: 62.3 us -> 58.9 us (0.945)
  Pallas kernels: 61.5 us -> 58 us
    pallas_call x1, Pallas kernels: 59.4 us -> 55.9 us  [owned_step(): pl.pallas_call(step_kernel, name='owned_step', out_shape=(jax.ShapeDtypeS...]
where the time goes in v2:
time: 58.9 us; the launch traced here: 58.6 us
  Pallas kernels  58 us (98%)
  between operations  0.65 us (1%)
    pallas_call x1, Pallas kernels, owned_step(): pl.pallas_call(step_kernel, name='owned_step', out_shape=(jax.ShapeDtypeS...  55.9 us
    pallas_call x1, Pallas kernels, place_rows(): pl.pallas_call(place_kernel, name='place_rows', out_shape=(jax.ShapeDtype...  2.09 us

profile of v2, /device:TPU:0, one launch (start us, length us, event | category | flops | bytes accessed | tf_op | source)
XLA Modules:
  0.0 58.6 jit_solution(14746144876872379991)
XLA Ops:
  0.6 0.0 copy-start
  0.6 55.9 %owned_step.1 = (bf16[8,64,512]{2,1,0:T(8,128)(2,1)S(1)}, f32[2,512,512]{2,1,0:T(8,128)S(1)}) custom-call(s32[8]{0:T(128)} %owner_ref.1, bf16[256,4096]{1,0:T(8,128)(2,1)} %acts_ref.1, bf16[256,512]{1,0:T(8,128)(2,1)} %cot_ref.1, f32[2,512,512]{2,1,0:T(8,128)} %bitcast.2), custom_call_target="tpu_custom_call" | custom-call | tf_op jit(solution)/shard_map/owned_step/pallas_call | solution.py:420
  56.5 0.0 copy-done
  56.5 2.1 %place_rows.1 = (bf16[8,64,512]{2,1,0:T(8,128)(2,1)}, f32[2,512,512]{2,1,0:T(8,128)}) custom-call(s32[8]{0:T(128)S(1)} %copy-done, bf16[8,64,512]{2,1,0:T(8,128)(2,1)S(1)} %get-tuple-element.6.held_ref, f32[2,512,512]{2,1,0:T(8,128)S(1)} %get-tuple-element.7.pair_ref), custom_call_target="tpu_custom_call" | custom-call | tf_op jit(solution)/shard_map/place_rows/pallas_call | solution.py:459
Async XLA Ops:
  0.6 55.9 %copy-start = (s32[8]{0:T(128)S(1)}, s32[8]{0:T(128)}, u32[]{:S(2)}) copy-start(s32[8]{0:T(128)} %owner_ref.1) | copy-start | bytes 100

commit v3 on v2

--- a/solution.py
+++ b/solution.py
@@ -138,8 +138,8 @@
     return jnp.dot(former, latter, preferred_element_type=jnp.float32)
 
 
-def step_kernel(slot_ref, acts_ref, cot_ref, stat_ref, held_ref, new_ref,
-                stage, quarters, wholes, acts_all, cot_all, total, stats, direction, left_root,
+def step_kernel(slot_ref, acts_ref, cot_ref, stat_ref, out_ref, new_ref,
+                stage, quarters, wholes, acts_all, cot_all, total, stats, direction, left_root, held_ref,
                 a_send, a_recv, sib_send, sib_recv, y_send, y_recv, fwd_send, fwd_recv,
                 own_send, z_send, x_send, c_recv, quarter_sem, whole_sem, cot_sem, stat_sem,
                 back_send, back_recv, owner_ref, owner_sem):
@@ -350,6 +350,8 @@
             side_out(s, side).wait_send()
     for d in others:
         arrived(held_ref.at[d], back_recv.at[d])
+    for w in range(dp_count):
+        out_ref[w] = held_ref[owner_ref[w]]
     for copy in copies:
         copy.wait_send()
 
@@ -434,6 +436,7 @@
             pltpu.VMEM(stat_pair.shape, jnp.float32),
             pltpu.VMEM((blk, blk), low),
             pltpu.VMEM((blk, blk), low),
+            pltpu.VMEM((dp_count, blk // dp_count, blk), low),
         ] + [dma((dp_count,))] * 8 + [dma((3, CHUNKS)), dma((DEPTH, CHUNKS)), dma((DEPTH, CHUNKS)),
                                      dma((dp_count, CHUNKS)), dma((dp_count,)), dma((dp_count,)), dma, dma,
                                      dma((dp_count,)), dma((dp_count,)),
@@ -443,35 +446,32 @@
     )(*[pltpu.with_memory_space_constraint(a, pltpu.HBM) for a in (owner_slot, acts, cotangent, stat_pair)])
 
 
-def place_kernel(owner_ref, held_ref, pair_ref, out_ref, new_ref, sems, pair_sem):
-    stats_out = pltpu.make_async_copy(pair_ref, new_ref, pair_sem)
-    stats_out.start()
-    copies = [pltpu.make_async_copy(held_ref.at[owner_ref[w]], out_ref.at[w], sems.at[w])
-              for w in range(held_ref.shape[0])]
+def place_kernel(rows_ref, pair_ref, out_ref, new_ref, rows_sem, pair_sem):
+    copies = [pltpu.make_async_copy(pair_ref, new_ref, pair_sem), pltpu.make_async_copy(rows_ref, out_ref, rows_sem)]
     for copy in copies:
         copy.start()
-    for copy in copies + [stats_out]:
+    for copy in copies:
         copy.wait()
 
 
-def place_rows(owner_slot, held, new_pair):
+def place(rows, new_pair):
     vmem, hbm = pl.BlockSpec(memory_space=pltpu.VMEM), pl.BlockSpec(memory_space=pltpu.HBM)
     return pl.pallas_call(
         place_kernel,
-        name="place_rows",
-        out_shape=(jax.ShapeDtypeStruct(held.shape, held.dtype),
+        name="place",
+        out_shape=(jax.ShapeDtypeStruct(rows.shape, rows.dtype),
                    jax.ShapeDtypeStruct(new_pair.shape, new_pair.dtype)),
-        in_specs=[pl.BlockSpec(memory_space=pltpu.SMEM), vmem, vmem],
+        in_specs=[vmem, vmem],
         out_specs=(hbm, hbm),
-        scratch_shapes=[pltpu.SemaphoreType.DMA((held.shape[0],)), pltpu.SemaphoreType.DMA],
+        scratch_shapes=[pltpu.SemaphoreType.DMA, pltpu.SemaphoreType.DMA],
         compiler_params=pltpu.CompilerParams(vmem_limit_bytes=4 * 1024 * 1024),
-    )(owner_slot, held, new_pair)
+    )(rows, new_pair)
 
 
 def full_house(acts, cotangent, stats, owner_slot):
     dp_count, mp_count = lax.axis_size("dp"), lax.axis_size("mp")
-    held, new_pair = owned_step(owner_slot, acts, cotangent, stats[0, 0], dp_count, mp_count)
-    update, new_pair = place_rows(owner_slot, held, new_pair)
+    rows, new_pair = owned_step(owner_slot, acts, cotangent, stats[0, 0], dp_count, mp_count)
+    update, new_pair = place(rows, new_pair)
     return update, new_pair[None, None]
 
 

time: 58.9 us -> 58.3 us (0.990)
  Pallas kernels: 58 us -> 57.4 us
    pallas_call x1, Pallas kernels: 2.09 us -> 1.5 us  [place(): pl.pallas_call(place_kernel, name='place', out_shape=(jax.ShapeDtypeStruc...]
where the time goes in v3:
time: 58.3 us; the launch traced here: 58.1 us
  Pallas kernels  57.4 us (98%)
  between operations  0.64 us (1%)
    pallas_call x1, Pallas kernels, owned_step(): pl.pallas_call(step_kernel, name='owned_step', out_shape=(jax.ShapeDtypeS...  55.9 us
    pallas_call x1, Pallas kernels, place(): pl.pallas_call(place_kernel, name='place', out_shape=(jax.ShapeDtypeStruc...  1.5 us

profile of v3, /device:TPU:0, one launch (start us, length us, event | category | flops | bytes accessed | tf_op | source)
XLA Modules:
  0.0 58.1 jit_solution(10744893005746967802)
XLA Ops:
  0.6 55.9 %owned_step.1 = (bf16[8,64,512]{2,1,0:T(8,128)(2,1)S(1)}, f32[2,512,512]{2,1,0:T(8,128)S(1)}) custom-call(s32[8]{0:T(128)} %slot_ref.1, bf16[256,4096]{1,0:T(8,128)(2,1)} %acts_ref.1, bf16[256,512]{1,0:T(8,128)(2,1)} %cot_ref.1, f32[2,512,512]{2,1,0:T(8,128)} %bitcast.2), custom_call_target="tpu_custom_call" | custom-call | tf_op jit(solution)/shard_map/owned_step/pallas_call | solution.py:422
  56.6 1.5 %place.1 = (bf16[8,64,512]{2,1,0:T(8,128)(2,1)}, f32[2,512,512]{2,1,0:T(8,128)}) custom-call(bf16[8,64,512]{2,1,0:T(8,128)(2,1)S(1)} %get-tuple-element.6.rows_ref, f32[2,512,512]{2,1,0:T(8,128)S(1)} %get-tuple-element.7.pair_ref), custom_call_target="tpu_custom_call" | custom-call | tf_op jit(solution)/shard_map/place/pallas_call | solution.py:459
